TPU v7x, 64 devices: a 2x2x8 block of a 4x4x8 slice. The times are simulated.
64 devices in a mesh: dp: 4 (over x, y), tp: 16 (over z, core).
Axes of the slice: x: 2, y: 2, z: 8, core: 2. Of those that a mesh axis runs over, the one named last changes fastest.
The devices are a block of a 4x4x8 slice.
Arguments:
- ids: int32 [32, 256], P('dp'), parts along dimension 0
- E: bfloat16 [2048, 4096], P(None, 'tp')
- g: bfloat16 [4096], replicated
- W: bfloat16 [4096, 12288], P(None, 'tp')
- du: bfloat16 [32, 256, 12288], P('dp', None, 'tp'), parts along dimension 0
- dres: bfloat16 [32, 256, 4096], P('dp', 'tp'), parts along dimension 0
Outputs:
- output 1: bfloat16 [32, 256, 12288], P('dp', None, 'tp'), parts along dimension 0
- output 2: bfloat16 [32, 256, 4096], P('dp', 'tp'), parts along dimension 0
- output 3: float32 [8192, 4096], P('dp', 'tp'), parts along dimension 0
- output 4: float32 [16384, 12288], P('dp', 'tp'), parts along dimension 0
- output 5: float32 [16384], P('dp'), parts along dimension 0
There are 4 independent parts. A program takes and returns all parts, laid end to end along the dimension named above; an argument that names none is the same for every part.
All inputs are finite; a program needn't handle non-finite values.
Results may differ from a plain program's by a relative error of at most 0.00618159.
Values are sent between devices in bfloat16 or wider.
A program may use at most 768 MiB of HBM per device.

v0:
```python
import functools

import jax
import jax.numpy as jnp
from jax import lax
from jax.experimental import pallas as pl
from jax.experimental.layout import Layout, with_layout_constraint
from jax.experimental.pallas import tpu as pltpu
from jax.sharding import PartitionSpec as P


EPS = 1e-6
MESH = pl.DeviceIdType.MESH
f32 = jnp.float32
bf16 = jnp.bfloat16


def parts_kernel(nb, idx_ref, a_ref, b_ref, wa_ref, wb_ref, *outs):
    nt = (((1,), (1,)), ((), ()))
    o = (lax.dot_general(a_ref[...], wa_ref[...], nt, preferred_element_type=f32)
         + lax.dot_general(b_ref[...], wb_ref[...], nt, preferred_element_type=f32)).astype(outs[0].dtype)
    for i in range(nb):
        @pl.when(pl.program_id(0) == i)
        def _(i=i):
            outs[i][...] = o


def chip_parts(blocks, z, c, Z, C, a, b, W, Wo, dtype):
    blocks = sorted(blocks, key=lambda t: t[1])
    nb = len(blocks)
    N, FL = a.shape
    DL = Wo.shape[1]
    M = N // 2
    zd = [lax.rem(z + d + Z, Z) for d, _ in blocks]
    idx = jnp.stack([q * C + c for q in zd] + zd)
    first = sum(1 for _, h in blocks if h == 0)
    row = lambda i, s: (jnp.where(i >= first, 1, 0), 0)
    outs = pl.pallas_call(
        functools.partial(parts_kernel, nb),
        grid_spec=pltpu.PrefetchScalarGridSpec(
            num_scalar_prefetch=1,
            grid=(nb,),
            in_specs=[
                pl.BlockSpec((M, FL), row), pl.BlockSpec((M, FL), row),
                pl.BlockSpec((DL, FL), lambda i, s: (s[i], 0)), pl.BlockSpec((DL, FL), lambda i, s: (s[nb + i], 0)),
            ],
            out_specs=[pl.BlockSpec((M, DL), lambda i, s: (0, 0)) for _ in blocks],
        ),
        out_shape=[jax.ShapeDtypeStruct((M, DL), dtype) for _ in blocks],
        cost_estimate=pl.CostEstimate(flops=4 * M * DL * FL * nb, bytes_accessed=8 << 20, transcendentals=0),
        compiler_params=pltpu.CompilerParams(dimension_semantics=("arbitrary",), vmem_limit_bytes=40 << 20),
        name="chip_parts",
    )(idx, a, b, W, Wo.reshape(-1, FL))
    return dict(zip(blocks, outs))


def rowsum_kernel(ids_ref, du_ref, e_ref, hi_ref, lo_ref, x_ref, acc_ref):
    i = pl.program_id(0)
    vb = e_ref.shape[0]
    hot = lax.broadcasted_iota(jnp.int32, (vb, du_ref.shape[0]), 0) + i * vb == ids_ref[...]
    hot = jnp.where(hot, 1.0, 0.0).astype(bf16)
    d = jnp.dot(hot, du_ref[...], preferred_element_type=f32)
    hi = d.astype(bf16)
    hi_ref[...] = hi
    lo_ref[...] = (d - hi.astype(f32)).astype(bf16)
    x = lax.dot_general(hot, e_ref[...], (((0,), (0,)), ((), ())), preferred_element_type=f32)

    @pl.when(i == 0)
    def _():
        acc_ref[...] = x

    @pl.when(i > 0)
    def _():
        acc_ref[...] += x

    @pl.when(i == pl.num_programs(0) - 1)
    def _():
        x_ref[...] = acc_ref[...].astype(bf16)


def rowsums(ids, du, E):
    N, FL = du.shape
    V, DL = E.shape
    vb = 512
    one = pl.Buffered(1)
    return pl.pallas_call(
        rowsum_kernel,
        grid=(V // vb,),
        in_specs=[
            pl.BlockSpec((1, N), lambda i: (0, 0)),
            pl.BlockSpec((N, FL), lambda i: (0, 0), pipeline_mode=one),
            pl.BlockSpec((vb, DL), lambda i: (i, 0)),
        ],
        out_specs=[pl.BlockSpec((vb, FL), lambda i: (i, 0)), pl.BlockSpec((vb, FL), lambda i: (i, 0)),
                   pl.BlockSpec((N, DL), lambda i: (0, 0))],
        out_shape=[jax.ShapeDtypeStruct((V, FL), bf16), jax.ShapeDtypeStruct((V, FL), bf16),
                   jax.ShapeDtypeStruct((N, DL), bf16)],
        scratch_shapes=[pltpu.VMEM((N, DL), f32)],
        cost_estimate=pl.CostEstimate(flops=2 * V * N * (FL + DL), bytes_accessed=12 << 20, transcendentals=0),
        compiler_params=pltpu.CompilerParams(dimension_semantics=("arbitrary",), vmem_limit_bytes=40 << 20),
        name="rowsums",
    )(ids, du, E)


def send_all(G, s_ref, o_ref, send, recv):
    me = lax.axis_index('tp')
    bar = pltpu.get_barrier_semaphore()
    for k in range(1, G):
        pl.semaphore_signal(bar, inc=1, device_id={'tp': lax.rem(me + k, G)}, device_id_type=MESH)
    pl.semaphore_wait(bar, G - 1)
    copies = []
    for k in range(1, G):
        cp = pltpu.make_async_remote_copy(
            src_ref=s_ref, dst_ref=o_ref.at[me], send_sem=send.at[k - 1], recv_sem=recv.at[k - 1],
            device_id={'tp': lax.rem(me + k, G)}, device_id_type=MESH)
        cp.start()
        copies.append(cp)
    o_ref[me] = s_ref[...]
    return copies


def exchange_kernel(G, s_ref, o_ref, send, recv):
    for cp in send_all(G, s_ref, o_ref, send, recv):
        cp.wait()


def exchange(G, small):
    vm = pl.BlockSpec(memory_space=pltpu.VMEM)
    return pl.pallas_call(
        functools.partial(exchange_kernel, G),
        out_shape=jax.ShapeDtypeStruct((G,) + small.shape, f32),
        in_specs=[vm],
        out_specs=vm,
        scratch_shapes=[pltpu.SemaphoreType.DMA((G - 1,)), pltpu.SemaphoreType.DMA((G - 1,))],
        cost_estimate=pl.CostEstimate(flops=1 << 30, bytes_accessed=1 << 20, transcendentals=0),
        compiler_params=pltpu.CompilerParams(collective_id=1, has_side_effects=True, vmem_limit_bytes=4 << 20),
        name="exchange",
    )(small)


def tail_kernel(G, s_ref, ids_ref, q_ref, o_ref, d_ref, send, recv):
    copies = send_all(G, s_ref, o_ref, send, recv)
    N, Q = q_ref.shape
    DL = Q // 3
    vb = 512

    def block(i, carry):
        rows = pl.ds(pl.multiple_of(i * vb, vb), vb)
        hot = lax.broadcasted_iota(jnp.int32, (vb, N), 0) + i * vb == ids_ref[...]
        d3 = jnp.dot(jnp.where(hot, 1.0, 0.0).astype(bf16), q_ref[...], preferred_element_type=f32)
        d_ref[rows, :] = d3[:, :DL] + d3[:, DL:2 * DL] + d3[:, 2 * DL:]
        return carry

    lax.fori_loop(0, d_ref.shape[0] // vb, block, 0)
    for cp in copies:
        cp.wait()


def tail(G, V, small, ids, q):
    vm = pl.BlockSpec(memory_space=pltpu.VMEM)
    return pl.pallas_call(
        functools.partial(tail_kernel, G),
        out_shape=(jax.ShapeDtypeStruct((G,) + small.shape, f32), jax.ShapeDtypeStruct((V, q.shape[1] // 3), f32)),
        in_specs=[vm, vm, vm],
        out_specs=(vm, vm),
        scratch_shapes=[pltpu.SemaphoreType.DMA((G - 1,)), pltpu.SemaphoreType.DMA((G - 1,))],
        cost_estimate=pl.CostEstimate(flops=2 * V * q.shape[0] * q.shape[1], bytes_accessed=6 << 20, transcendentals=0),
        compiler_params=pltpu.CompilerParams(collective_id=0, has_side_effects=True, vmem_limit_bytes=40 << 20),
        name="tail",
    )(small, ids, q)


def forward_kernel(last, DP, *refs):
    if last:
        (eb_ref, rs_ref, g_ref, w_ref, dh_ref, dl_ref, sr_ref, up_ref, ids_ref, _,
         dw_ref, xo_ref, u_ref, acc_ref, ub_ref) = refs
    else:
        (eb_ref, rs_ref, g_ref, w_ref, dh_ref, dl_ref, sr_ref, dw_ref, xo_ref, acc_ref) = refs
    j = pl.program_id(0)
    x = jnp.concatenate([eb_ref[i, 0] for i in range(DP)], axis=1)
    n = (x.astype(f32) * rs_ref[...] * g_ref[...]).astype(bf16)
    dw_ref[...] = (jnp.dot(n, dh_ref[...], preferred_element_type=f32)
                   + jnp.dot(n, dl_ref[...], preferred_element_type=f32))
    xo_ref[...] = jnp.dot(x, sr_ref[...], preferred_element_type=f32).T.astype(bf16)
    up = lax.dot_general(w_ref[...], n, (((0,), (0,)), ((), ())), preferred_element_type=f32)

    @pl.when(j == 0)
    def _():
        acc_ref[...] = up + up_ref[...] if last else up

    @pl.when(j > 0)
    def _():
        acc_ref[...] += up

    if last:
        @pl.when(j == pl.num_programs(0) - 1)
        def _():
            ub_ref[...] = acc_ref[...].astype(bf16)
            tb = 512

            def step(i, carry):
                rows = pl.ds(pl.multiple_of(i * tb, tb), tb)
                V = ub_ref.shape[1]
                hot = lax.broadcasted_iota(jnp.int32, (tb, V), 1) == ids_ref[rows, :]
                s = jnp.where(hot, 1.0, 0.0).astype(bf16)
                u_ref[rows, :] = lax.dot_general(s, ub_ref[...], (((1,), (1,)), ((), ())),
                                                 preferred_element_type=f32).astype(bf16)
                return carry

            lax.fori_loop(0, u_ref.shape[0] // tb, step, 0)


def forward(q, eb, rs, gcol, W, dh, dl, sr, up=None, ids=None, dw=None):
    last = q == 1
    DP, C, _, Vp = eb.shape
    V = DP * Vp
    D, FL = W.shape
    Dq = D // (2 * C)
    kt = 512
    nk = Dq // kt
    TS = sr.shape[1]
    base = q * C * nk
    one = pl.Buffered(1)

    def full(shape):
        return pl.BlockSpec(shape, lambda j: (0,) * len(shape), pipeline_mode=one)

    in_specs = [
        pl.BlockSpec((DP, 1, kt, Vp), lambda j: (0, j // nk, j % nk, 0)),
        full((1, V)),
        pl.BlockSpec((kt, 1), lambda j: (base + j, 0)),
        pl.BlockSpec((kt, FL), lambda j: (base + j, 0)),
        full((V, FL)), full((V, FL)), full((V, TS)),
    ]
    args = [eb, rs, gcol, W, dh, dl, sr]
    out_shape = [jax.ShapeDtypeStruct((D, FL), f32), jax.ShapeDtypeStruct((TS, D // 2), bf16)]
    out_specs = [pl.BlockSpec((kt, FL), lambda j: (base + j, 0)), pl.BlockSpec((TS, kt), lambda j: (0, j))]
    scratch = []
    alias = {}
    if last:
        N = ids.shape[0]
        in_specs += [full((FL, V)), full((N, 1)), pl.BlockSpec(memory_space=pl.ANY)]
        args += [up, ids, dw]
        alias = {9: 0}
        out_shape.append(jax.ShapeDtypeStruct((N, FL), bf16))
        out_specs.append(full((N, FL)))
        scratch = [pltpu.VMEM((FL, V), f32), pltpu.VMEM((FL, V), bf16)]
    else:
        out_shape.append(jax.ShapeDtypeStruct((FL, V), f32))
        out_specs.append(full((FL, V)))
    flops = 2 * V * FL * (D // 2) * 3 + (2 * V * V * FL if last else 0)
    return pl.pallas_call(
        functools.partial(forward_kernel, last, DP),
        grid=(C * nk,),
        in_specs=in_specs,
        out_specs=out_specs,
        out_shape=out_shape,
        scratch_shapes=scratch,
        input_output_aliases=alias,
        cost_estimate=pl.CostEstimate(flops=flops, bytes_accessed=30 << 20, transcendentals=0),
        compiler_params=pltpu.CompilerParams(dimension_semantics=("arbitrary",), vmem_limit_bytes=(52 if last else 40) << 20),
        name="forward",
    )(*args)


barrier = lax.optimization_barrier


def rows(a):
    return with_layout_constraint(a, Layout(major_to_minor=(0, 1)))


def split3(a):
    hi = lax.reduce_precision(a, 8, 7)
    mi = lax.reduce_precision(a - hi, 8, 7)
    lo = a - hi - mi
    return hi.astype(bf16), mi.astype(bf16), lo.astype(bf16)


def solution(mesh):
    G = mesh.shape['tp']
    DP = mesh.shape['dp']
    C = 2
    Z = G // C
    groups = [[d * G + z * C + c for d in range(DP) for c in range(C)] for z in range(Z)]

    def shift(k):
        return [(z * C + c, ((z + k) % Z) * C + c) for z in range(Z) for c in range(C)]

    swap = [(i, i ^ 1) for i in range(G)]

    def program(ids, E, g, W, du, dres):
        K, T = ids.shape
        N = K * T
        V, DL = E.shape
        D = g.shape[0]
        FL = W.shape[1]
        TL = T // G
        Vp = V // DP
        Dq = D // (2 * C)
        r = lax.axis_index('tp')
        grp = lax.axis_index('dp')
        z = r // C
        c = r % C
        gf = g.astype(f32)
        idf = ids.reshape(N)

        duf = du.reshape(N, FL)
        iota = jnp.arange(V, dtype=jnp.int32)

        Ep = lax.dynamic_slice_in_dim(E, grp * Vp, Vp, axis=0)
        AT = lax.all_gather(rows(Ep.T), 'tp', axis=0, tiled=True)

        du_o = lax.ppermute(duf, 'tp', swap)
        Ws = lax.dynamic_index_in_dim(W.reshape(Z, C, DL, FL), 1 - c, 1, False)
        W_o = lax.ppermute(Ws, 'tp', swap)
        gcol = gf.reshape(D, 1)
        du_o, W_o, gcol = barrier((du_o, W_o, gcol))
        F = Z // 2

        streams = [(0, 1, F), (1, -1, F), (1, 1, F - 1), (0, -1, F - 1)]
        acc = {0: [], 1: []}

        def hop(bufs):
            out = {}
            for st, b in bufs.items():
                out[st] = lax.ppermute(b, 'tp', shift(st[1]))
            return out

        def blocks(k):
            return [(s * (L - k), h) for h, s, L in streams if k < L]

        def add(moved, k, parts, hook):
            nxt = {}
            for (h, s, L), b in moved.items():
                if k == L:
                    acc[h].append(b)
                else:
                    b, _ = barrier((b, hook))
                    nxt[(h, s, L)] = b.astype(f32) + parts[(s * (L - k), h)]
            return nxt

        def chip(bl, Wo, dtype):
            return chip_parts(bl, z, c, Z, C, duf, du_o, W, Wo, dtype)

        p = chip(blocks(0), W_o, bf16)
        bufs = {(h, s, L): p[(s * L, h)] for h, s, L in streams}
        moved = hop(bufs)
        Wo1, _ = barrier((W_o, tuple(bufs.values())))
        p2 = chip(blocks(1), Wo1, f32)

        el = E.astype(f32)
        ssl = jnp.sum(el * el, axis=1)
        ssl, _ = barrier((ssl, tuple(p2.values())))
        ssg = exchange(G, ssl.reshape(V // 128, 128))
        rs2 = lax.rsqrt(jnp.sum(ssg, axis=0) / D + EPS).reshape(1, V)

        b1 = lax.dynamic_slice_in_dim(AT, c * Dq, Dq, axis=0)
        b2 = lax.dynamic_slice_in_dim(AT, D // 2 + c * Dq, Dq, axis=0)
        b1, b2 = barrier((rows(b1), rows(b2)))
        e1 = lax.all_gather(b1, ('dp', 'tp'), axis_index_groups=groups, axis=0, tiled=False).reshape(DP, C, Dq, Vp)
        e2 = lax.all_gather(b2, ('dp', 'tp'), axis_index_groups=groups, axis=0, tiled=False).reshape(DP, C, Dq, Vp)

        bufs = add(moved, 1, p2, b2)
        Wo2, _ = barrier((W_o, tuple(bufs.values())))
        moved = hop(bufs)
        p3 = chip([t for k in range(2, F) for t in blocks(k)] + [(0, 0), (0, 1)], Wo2, f32)
        idx, _ = barrier((idf, tuple(p3.values())))
        dh, dl, xl = rowsums(idx.reshape(1, N), duf, E)
        rst = jnp.sum(jnp.where(idx[:, None] == iota[None, :], rs2, 0.0), axis=1)
        idr = lax.dynamic_slice_in_dim(ids, r * TL, TL, axis=1).reshape(K * TL)
        sr = (iota[:, None] == idr[None, :]).astype(bf16)
        idc = idx.reshape(N, 1)
        rs2, sr, idc, xl, rst = barrier((rs2, sr, idc, xl, rst))

        bufs = add(moved, 2, p3, xl)
        rs2, _ = barrier((rs2, tuple(bufs.values())))
        moved = hop(bufs)
        drs, _ = barrier((dres, tuple(bufs.values())))
        dc = lax.all_to_all(drs.reshape(K, TL, G, DL), 'tp', 2, 0, tiled=False)
        dresc = dc.reshape(G, K, TL, DL).transpose(1, 0, 2, 3).reshape(N, DL)
        dw1, x1, up = forward(0, e1, rs2, gcol, W, dh, dl, sr)
        for k in range(3, F):
            bufs = add(moved, k, p3, x1)
            rs2, _ = barrier((rs2, tuple(bufs.values())))
            moved = hop(bufs)
        dW, x2, u = forward(1, e2, rs2, gcol, W, dh, dl, sr, up, idc, dw1)
        moved = {st: barrier((b, x2))[0] for st, b in moved.items()}
        add(moved, F, p3, x2)
        dn = jnp.concatenate([p3[(0, h)] + sum(b.astype(f32) for b in acc[h]) for h in (0, 1)], axis=0)
        xo = jnp.concatenate([x1, x2], axis=1).reshape(K, TL, D)
        u = u.reshape(K, T, FL)

        gl = lax.dynamic_slice_in_dim(gf, r * DL, DL)
        nh = xl.astype(f32) * rst[:, None]
        gdn = gl * dn
        sp = jnp.sum(nh * gdn, axis=1)
        dgl = jnp.sum(dn * nh, axis=0)
        small = jnp.concatenate([sp, dgl]).reshape((N + DL) // 128, 128)
        q = jnp.concatenate(split3(dresc.astype(f32) + rst[:, None] * gdn), axis=1)
        small, dA = tail(G, V, small, idx.reshape(1, N), q)
        small = small.reshape(G, N + DL)
        s = jnp.sum(small[:, :N], axis=0) / D
        dg = small[:, N:].reshape(D)
        sv = jnp.sum(jnp.where(iota[:, None] == idf[None, :], s[None, :], 0.0), axis=1)
        rv = rs2.reshape(V, 1)
        dE = dA - rv * (E.astype(f32) * rv) * sv[:, None]
        return u, xo, dE, dW, dg

    return jax.shard_map(
        program,
        mesh=mesh,
        in_specs=(P('dp', None), P(None, 'tp'), P(), P(None, 'tp'), P('dp', None, 'tp'), P('dp', 'tp', None)),
        out_specs=(P('dp', None, 'tp'), P('dp', 'tp', None), P('dp', 'tp'), P('dp', 'tp'), P('dp')),
        check_vma=False,
    )
```

profile of v0, /device:TPU:21, one launch (start us, length us, event | category | flops | bytes accessed | tf_op | source)
XLA Modules:
  0.0 314.3 jit_solution(998990350054622261)
XLA Ops:
  9.2 44.8 %all-gather.6.cloned.1.call-done = bf16[4096,512]{1,0:T(8,128)(2,1)} async-done(((bf16[256,512]{1,0:T(8,128)(2,1)}), bf16[4096,512]{1,0:T(8,128)(2,1)}) %all-gather.6.cloned.1.call-update) | async-done | bytes 4194320 | tf_op jit(solution)/shard_map/all_gather | solution.py:312
  54.0 3.0 constant_dynamic-slice_fusion.1
  57.9 3.9 %dynamic-slice_bitcast_fusion = bf16[8,256,768]{2,1,0:T(8,128)(2,1)} fusion(bf16[8,2,256,768]{3,2,1,0:T(8,128)(2,1)} %bitcast.80, s32[]{:T(128)S(6)} %select_n.42), kind=kLoop, calls=%fused_computation.5 | loop fusion | bytes 6291460 | tf_op jit(solution)/shard_map/jit(dynamic_index_in_dim)/squeeze | solution.py:315
  62.8 1.6 fusion
  65.3 2.5 collective-permute-done.1
  67.8 4.5 %collective-permute-done.b_ref = bf16[2048,768]{1,0:T(8,128)(2,1)} collective-permute-done((bf16[2048,768]{1,0:T(8,128)(2,1)S(1)}, bf16[2048,768]{1,0:T(8,128)(2,1)}, u32[]{:S(2)}, u32[]{:S(2)}) %collective-permute-start) | collective-permute-done | bytes 3145760 | tf_op jit(solution)/shard_map/ppermute | solution.py:314
  72.3 8.3 %chip_parts.3 = (bf16[1024,256]{1,0:T(8,128)(2,1)}, bf16[1024,256]{1,0:T(8,128)(2,1)}, bf16[1024,256]{1,0:T(8,128)(2,1)}, bf16[1024,256]{1,0:T(8,128)(2,1)}) custom-call(s32[8]{0:T(128)S(1)} %stack.90.idx_ref, bf16[2048,768]{1,0:T(8,128)(2,1)S(1)} %bitcast.66, bf16[2048,768]{1,0:T(8,128)(2,1)} %collective-permute-done.b_ref, bf16[4096,768]{1,0:T(8,128)(2,1)} %refs_3_.3, ...), custom_call_target="tpu_custom_call" | custom-call | flops 3221225472 | bytes 8388608 | tf_op jit(solution)/shard_map/chip_parts/pallas_call | solution.py:38
  80.7 1.8 collective-permute-start.5
  82.5 2.7 collective-permute-start.3
  85.2 7.2 %chip_parts.4 = (f32[1024,256]{1,0:T(8,128)S(1)}, f32[1024,256]{1,0:T(8,128)S(1)}, f32[1024,256]{1,0:T(8,128)S(1)}, f32[1024,256]{1,0:T(8,128)S(1)}) custom-call(s32[8]{0:T(128)S(1)} %stack.85.idx_ref, bf16[2048,768]{1,0:T(8,128)(2,1)S(1)} %bitcast.67, bf16[2048,768]{1,0:T(8,128)(2,1)} %collective-permute-done.b_ref, bf16[4096,768]{1,0:T(8,128)(2,1)} %refs_3_.3, ...), custom_call_target="tpu_custom_call" | custom-call | flops 3221225472 | bytes 8388608 | tf_op jit(solution)/shard_map/chip_parts/pallas_call | solution.py:38
  96.3 15.5 %exchange.1 = f32[16,16,128]{2,1,0:T(8,128)S(1)} custom-call(f32[16,128]{1,0:T(8,128)S(1)} %bitcast.79), custom_call_target="tpu_custom_call" | custom-call | flops 1073741824 | bytes 1048576 | tf_op jit(solution)/shard_map/exchange/pallas_call | solution.py:129
  111.9 1.7 convert_add_fusion
  113.9 1.2 convert_add_fusion.1
  115.1 1.4 collective-permute-start.8
  116.5 1.1 convert_add_fusion.2
  117.7 2.4 collective-permute-start.7
  120.0 1.1 convert_add_fusion.3
  121.6 12.0 %chip_parts.5 = (f32[1024,256]{1,0:T(8,128)S(1)}, f32[1024,256]{1,0:T(8,128)S(1)}, f32[1024,256]{1,0:T(8,128)S(1)}, f32[1024,256]{1,0:T(8,128)S(1)}, f32[1024,25...) custom-call(s32[16]{0:T(128)S(1)} %stack.97.idx_ref, ...), custom_call_target="tpu_custom_call" | custom-call | flops 6442450944 | bytes 8388608 | tf_op jit(solution)/shard_map/chip_parts/pallas_call | solution.py:38
  137.6 2.3 select_reduce_fusion.1
  139.8 10.3 %rowsums.1 = (bf16[2048,768]{1,0:T(8,128)(2,1)S(1)}, bf16[2048,768]{1,0:T(8,128)(2,1)S(1)}, bf16[2048,256]{1,0:T(8,128)(2,1)S(1)}) custom-call(s32[1,2048]{1,0:T(1,128)S(1)} %bitcast.75, bf16[2048,768]{1,0:T(8,128)(2,1)S(1)} %bitcast.69, bf16[2048,256]{1,0:T(8,128)(2,1)S(1)} %copy-done.1), custom_call_target="tpu_custom_call" | custom-call | flops 8589934592 | bytes 12582912 | tf_op jit(solution)/shard_map/rowsums/pallas_call | solution.py:86
  150.2 1.7 copy-done.24
  151.9 1.2 add.223
  153.1 1.4 add.222
  154.6 6.2 %collective-permute-done.7 = f32[1024,256]{1,0:T(8,128)S(1)} collective-permute-done((f32[1024,256]{1,0:T(8,128)S(1)}, f32[1024,256]{1,0:T(8,128)S(1)}, u32[]{:S(2)}, u32[]{:S(2)}) %collective-permute-start.7) | collective-permute-done | bytes 1048608 | tf_op jit(solution)/shard_map/ppermute | solution.py:327
  160.7 1.1 add.221
  161.8 2.4 collective-permute-done.6
  164.2 1.1 add.220
  165.6 1.3 copy.34
  166.9 5.2 %all-to-all-start = ((bf16[1,8,16,16,256]{4,2,1,0,3:T(8,128)(2,1)}), bf16[1,8,16,16,256]{4,2,1,0,3:T(8,128)(2,1)}, u32[]{:S(2)}, u32[]{:S(2)}) async-start(bf16[1,8,16,16,256]{4,2,1,0,3:T(8,128)(2,1)} %copy.34), calls=%async_computation | async-start | bytes 2097152 | tf_op jit(solution)/shard_map/all_to_all | solution.py:380
  172.8 1.7 copy.33.refs_8_
  174.5 2.8 collective-permute-start.11
  177.4 2.7 collective-permute-start.12
  180.6 19.7 %all-to-all-done = bf16[1,8,16,16,256]{4,2,1,0,3:T(8,128)(2,1)} async-done(((bf16[1,8,16,16,256]{4,2,1,0,3:T(8,128)(2,1)}), bf16[1,8,16,16,256]{4,2,1,0,3:T(8,128)(2,1)}, u32[]{:S(2)}, u32[]{:S(2)}) %all-to-all-start) | async-done | bytes 1048608 | tf_op jit(solution)/shard_map/all_to_all | solution.py:380
  200.3 1.5 convert_bitcast_fusion
  201.8 1.5 copy.35
  203.3 1.9 copy-done.23
  205.2 1.9 copy-done.25
  207.1 30.0 %forward.2 = (f32[4096,768]{1,0:T(8,128)}, bf16[128,2048]{1,0:T(8,128)(2,1)S(1)}, f32[768,2048]{1,0:T(8,128)}) custom-call(bf16[4,2,1024,512]{3,2,1,0:T(8,128)(2,1)} %bitcast.91, f32[1,2048]{1,0:T(1,128)S(1)} %bitcast.71, f32[4096,1]{1,0:T(8,128)S(1)} %copy.31.refs_2_, bf16[4096,768]{1,0:T(8,128)(2,1)} %refs_3_.3, bf16[2048,768]{1,0:T(8,128)(2,1)S(1)} %copy-done.23, ...), custom_call_target="tpu_custom_call" | custom-call | flops 19327352832 | bytes 31457280 | tf_op jit(solution)/shard_map/forward/pallas_call | solution.py:252
  237.1 2.5 add.225
  239.6 2.4 add.224
  242.0 2.8 collective-permute-start.15
  244.8 41.0 %forward.3 = (f32[4096,768]{1,0:T(8,128)}, bf16[128,2048]{1,0:T(8,128)(2,1)S(1)}, bf16[2048,768]{1,0:T(8,128)(2,1)}) custom-call(bf16[4,2,1024,512]{3,2,1,0:T(8,128)(2,1)} %bitcast.90, f32[1,2048]{1,0:T(1,128)S(1)} %bitcast.72, f32[4096,1]{1,0:T(8,128)} %copy-done.3, bf16[4096,768]{1,0:T(8,128)(2,1)} %refs_3_.3, ...), custom_call_target="tpu_custom_call", output_to_operand_aliasing={{0}: (9, {})} | custom-call | flops 25769803776 | bytes 31457280 | tf_op jit(solution)/shard_map/forward/pallas_call | solution.py:252
  286.9 1.7 add_add_fusion.1
  288.7 1.9 add_add_fusion
  291.2 1.2 reduce-precision_convert_fusion.1
  293.0 10.3 %tail.1 = (f32[16,18,128]{2,1,0:T(8,128)S(1)}, f32[2048,256]{1,0:T(8,128)S(1)}) custom-call(f32[18,128]{1,0:T(8,128)S(1)} %maximum_bitcast_fusion.s_ref, s32[1,2048]{1,0:T(1,128)S(1)} %bitcast.77, bf16[2048,768]{1,0:T(8,128)(2,1)S(1)} %pad_maximum_fusion.q_ref), custom_call_target="tpu_custom_call" | custom-call | flops 6442450944 | bytes 6291456 | tf_op jit(solution)/shard_map/tail/pallas_call | solution.py:161
  303.5 1.7 select_reduce_fusion
  305.9 1.7 fusion.3
  (110 shorter events, 18.0 us)
Async XLA Ops:
  7.2 46.9 %all-gather.6.cloned.1.call-start = ((), (), s32[]{:S(2)}) async-start(), calls=%async_computation.1 | async-start | bytes 4456448 | tf_op jit(solution)/shard_map/all_gather | solution.py:312
  9.1 194.2 %all-gather.10.cloned.1.call-start = ((), (), s32[]{:S(2)}) async-start(), calls=%async_computation.3 | async-start | bytes 9437184 | tf_op jit(solution)/shard_map/all_gather | solution.py:361
  57.1 187.7 %all-gather.8.cloned.1.call-start = ((), (), s32[]{:S(2)}) async-start(), calls=%async_computation.2 | async-start | bytes 9437184 | tf_op jit(solution)/shard_map/all_gather | solution.py:362
  57.9 4.2 %copy-start = (bf16[8,256,768]{2,1,0:T(8,128)(2,1)S(1)}, bf16[8,256,768]{2,1,0:T(8,128)(2,1)}, u32[]{:S(2)}) copy-start(bf16[8,256,768]{2,1,0:T(8,128)(2,1)} %param.10) | copy-start | bytes 9437188
  57.9 4.5 %copy-start.29 = (bf16[4096]{0:T(1024)(128)(2,1)S(1)}, bf16[4096]{0:T(1024)(128)(2,1)}, u32[]{:S(2)}) copy-start(bf16[4096]{0:T(1024)(128)(2,1)} %param.8) | copy-start | bytes 24580
  57.9 4.4 %copy-start.28 = (s32[8,256]{1,0:T(8,128)S(1)}, s32[8,256]{1,0:T(8,128)}, u32[]{:S(2)}) copy-start(s32[8,256]{1,0:T(8,128)} %param.6) | copy-start | bytes 24580
  61.8 6.0 %collective-permute-start.1 = (bf16[8,256,768]{2,1,0:T(8,128)(2,1)}, bf16[8,256,768]{2,1,0:T(8,128)(2,1)}, u32[]{:S(2)}, u32[]{:S(2)}) collective-permute-start(bf16[8,256,768]{2,1,0:T(8,128)(2,1)} %dynamic-slice_bitcast_fusion), channel_id=1, source_target_pairs={{0,1},{1,0},{2,3},{3,2},{4,5},{5,4},{6,7},{7,6},{8,9},{9,8},{10,11... | collective-permute-start | bytes 9437192 | tf_op jit(solution)/shard_map/ppermute | solution.py:316
  62.1 10.2 %collective-permute-start = (bf16[2048,768]{1,0:T(8,128)(2,1)S(1)}, bf16[2048,768]{1,0:T(8,128)(2,1)}, u32[]{:S(2)}, u32[]{:S(2)}) collective-permute-start(bf16[2048,768]{1,0:T(8,128)(2,1)S(1)} %bitcast.65), channel_id=1, source_target_pairs={{0,1},{1,0},{2,3},{3,2},{4,5},{5,4},{6,7},{7,6},{8,9},{9,8},{10,11... | collective-permute-start | bytes 9437192 | tf_op jit(solution)/shard_map/ppermute | solution.py:314
  80.7 31.2 %collective-permute-start.5 = (bf16[1024,256]{1,0:T(8,128)(2,1)}, bf16[1024,256]{1,0:T(8,128)(2,1)}, u32[]{:S(2)}, u32[]{:S(2)}) collective-permute-start(bf16[1024,256]{1,0:T(8,128)(2,1)} %get-tuple-element.67), channel_id=1, source_target_pairs={{0,14},{1,15},{2,0},{3,1},{4,2},{5,3},{6,4},{7,5},{8,6},{9,7},{10,... | collective-permute-start | bytes 1572872 | tf_op jit(solution)/shard_map/ppermute | solution.py:327
  82.5 29.4 %collective-permute-start.4 = (bf16[1024,256]{1,0:T(8,128)(2,1)}, bf16[1024,256]{1,0:T(8,128)(2,1)}, u32[]{:S(2)}, u32[]{:S(2)}) collective-permute-start(bf16[1024,256]{1,0:T(8,128)(2,1)} %get-tuple-element.66), channel_id=1, source_target_pairs={{0,2},{1,3},{2,4},{3,5},{4,6},{5,7},{6,8},{7,9},{8,10},{9,11},{10,... | collective-permute-start | bytes 1572872 | tf_op jit(solution)/shard_map/ppermute | solution.py:327
  82.5 29.4 %collective-permute-start.3 = (bf16[1024,256]{1,0:T(8,128)(2,1)}, bf16[1024,256]{1,0:T(8,128)(2,1)}, u32[]{:S(2)}, u32[]{:S(2)}) collective-permute-start(bf16[1024,256]{1,0:T(8,128)(2,1)} %get-tuple-element.65), channel_id=1, source_target_pairs={{0,14},{1,15},{2,0},{3,1},{4,2},{5,3},{6,4},{7,5},{8,6},{9,7},{10,... | collective-permute-start | bytes 1572872 | tf_op jit(solution)/shard_map/ppermute | solution.py:327
  85.2 26.7 %collective-permute-start.2 = (bf16[1024,256]{1,0:T(8,128)(2,1)}, bf16[1024,256]{1,0:T(8,128)(2,1)}, u32[]{:S(2)}, u32[]{:S(2)}) collective-permute-start(bf16[1024,256]{1,0:T(8,128)(2,1)} %get-tuple-element.64), channel_id=1, source_target_pairs={{0,2},{1,3},{2,4},{3,5},{4,6},{5,7},{6,8},{7,9},{8,10},{9,11},{10,... | collective-permute-start | bytes 1572872 | tf_op jit(solution)/shard_map/ppermute | solution.py:327
  93.3 1.0 copy-start.12
  95.2 1.0 copy-start.16
  111.8 2.1 copy-start.15
  111.8 4.7 %copy-start.13 = (f32[1024,256]{1,0:T(8,128)S(1)}, f32[1024,256]{1,0:T(8,128)}, u32[]{:S(2)}) copy-start(f32[1024,256]{1,0:T(8,128)} %copy-done.12) | copy-start | bytes 3145732
  113.6 6.4 %copy-start.11 = (f32[1024,256]{1,0:T(8,128)S(1)}, f32[1024,256]{1,0:T(8,128)}, u32[]{:S(2)}) copy-start(f32[1024,256]{1,0:T(8,128)} %copy-done.10) | copy-start | bytes 3145732
  113.6 38.3 %collective-permute-start.9 = (f32[1024,256]{1,0:T(8,128)S(1)}, f32[1024,256]{1,0:T(8,128)S(1)}, u32[]{:S(2)}, u32[]{:S(2)}) collective-permute-start(f32[1024,256]{1,0:T(8,128)S(1)} %convert_add_fusion), channel_id=1, source_target_pairs={{0,14},{1,15},{2,0},{3,1},{4,2},{5,3},{6,4},{7,5},{8,6},{9,7},{10,... | collective-permute-start | bytes 3145736 | tf_op jit(solution)/shard_map/ppermute | solution.py:327
  115.1 38.0 %collective-permute-start.8 = (f32[1024,256]{1,0:T(8,128)S(1)}, f32[1024,256]{1,0:T(8,128)S(1)}, u32[]{:S(2)}, u32[]{:S(2)}) collective-permute-start(f32[1024,256]{1,0:T(8,128)S(1)} %convert_add_fusion.1), channel_id=1, source_target_pairs={{0,2},{1,3},{2,4},{3,5},{4,6},{5,7},{6,8},{7,9},{8,10},{9,11},{10,... | collective-permute-start | bytes 3145736 | tf_op jit(solution)/shard_map/ppermute | solution.py:327
  117.7 43.1 %collective-permute-start.7 = (f32[1024,256]{1,0:T(8,128)S(1)}, f32[1024,256]{1,0:T(8,128)S(1)}, u32[]{:S(2)}, u32[]{:S(2)}) collective-permute-start(f32[1024,256]{1,0:T(8,128)S(1)} %convert_add_fusion.2), channel_id=1, source_target_pairs={{0,14},{1,15},{2,0},{3,1},{4,2},{5,3},{6,4},{7,5},{8,6},{9,7},{10,... | collective-permute-start | bytes 3145736 | tf_op jit(solution)/shard_map/ppermute | solution.py:327
  121.2 43.0 %collective-permute-start.6 = (f32[1024,256]{1,0:T(8,128)S(1)}, f32[1024,256]{1,0:T(8,128)S(1)}, u32[]{:S(2)}, u32[]{:S(2)}) collective-permute-start(f32[1024,256]{1,0:T(8,128)S(1)} %convert_add_fusion.3), channel_id=1, source_target_pairs={{0,2},{1,3},{2,4},{3,5},{4,6},{5,7},{6,8},{7,9},{8,10},{9,11},{10,... | collective-permute-start | bytes 3145736 | tf_op jit(solution)/shard_map/ppermute | solution.py:327
  121.6 18.3 %copy-start.1 = (bf16[2048,256]{1,0:T(8,128)(2,1)S(1)}, bf16[2048,256]{1,0:T(8,128)(2,1)}, u32[]{:S(2)}) copy-start(bf16[2048,256]{1,0:T(8,128)(2,1)} %e_ref.1) | copy-start | bytes 3145732
  133.6 1.0 copy-start.6
  134.6 1.0 copy-start.8
  135.6 1.0 copy-start.17
  136.6 1.0 copy-start.19
  150.2 1.7 copy-start.24
  151.9 2.7 copy-start.4
  151.9 2.7 copy-start.22
  154.6 10.8 %copy-start.27 = (bf16[8,16,4096]{2,1,0:T(8,128)(2,1)S(1)}, bf16[8,16,4096]{2,1,0:T(8,128)(2,1)}, u32[]{:S(2)}) copy-start(bf16[8,16,4096]{2,1,0:T(8,128)(2,1)} %param.11) | copy-start | bytes 3145732
  166.9 33.4 %all-to-all-start = ((bf16[1,8,16,16,256]{4,2,1,0,3:T(8,128)(2,1)}), bf16[1,8,16,16,256]{4,2,1,0,3:T(8,128)(2,1)}, u32[]{:S(2)}, u32[]{:S(2)}) async-start(bf16[1,8,16,16,256]{4,2,1,0,3:T(8,128)(2,1)} %copy.34), calls=%async_computation | async-start | bytes 2097152 | tf_op jit(solution)/shard_map/all_to_all | solution.py:380
  172.8 30.5 %copy-start.3 = (f32[4096,1]{1,0:T(8,128)}, f32[4096,1]{1,0:T(8,128)S(1)}, u32[]{:S(2)}) copy-start(f32[4096,1]{1,0:T(8,128)S(1)} %copy.31.refs_2_) | copy-start | bytes 49156
  174.5 28.8 %copy-start.21 = (bf16[2048,128]{1,0:T(8,128)(2,1)S(1)}, bf16[2048,128]{1,0:T(8,128)(2,1)}, u32[]{:S(2)}) copy-start(bf16[2048,128]{1,0:T(8,128)(2,1)} %fusion.5.refs_6_) | copy-start | bytes 1572868
  174.5 62.6 %collective-permute-start.11 = (f32[1024,256]{1,0:T(8,128)}, f32[1024,256]{1,0:T(8,128)}, u32[]{:S(2)}, u32[]{:S(2)}) collective-permute-start(f32[1024,256]{1,0:T(8,128)} %add.221), channel_id=1, source_target_pairs={{0,14},{1,15},{2,0},{3,1},{4,2},{5,3},{6,4},{7,5},{8,6},{9,7},{10,... | collective-permute-start | bytes 3145736 | tf_op jit(solution)/shard_map/ppermute | solution.py:327
  177.4 62.2 %collective-permute-start.10 = (f32[1024,256]{1,0:T(8,128)}, f32[1024,256]{1,0:T(8,128)}, u32[]{:S(2)}, u32[]{:S(2)}) collective-permute-start(f32[1024,256]{1,0:T(8,128)} %add.220), channel_id=1, source_target_pairs={{0,2},{1,3},{2,4},{3,5},{4,6},{5,7},{6,8},{7,9},{8,10},{9,11},{10,... | collective-permute-start | bytes 3145736 | tf_op jit(solution)/shard_map/ppermute | solution.py:327
  177.4 109.5 %collective-permute-start.12 = (f32[1024,256]{1,0:T(8,128)}, f32[1024,256]{1,0:T(8,128)}, u32[]{:S(2)}, u32[]{:S(2)}) collective-permute-start(f32[1024,256]{1,0:T(8,128)} %add.223), channel_id=1, source_target_pairs={{0,14},{1,15},{2,0},{3,1},{4,2},{5,3},{6,4},{7,5},{8,6},{9,7},{10,... | collective-permute-start | bytes 3145736 | tf_op jit(solution)/shard_map/ppermute | solution.py:327
  180.1 108.6 %collective-permute-start.14 = (f32[1024,256]{1,0:T(8,128)}, f32[1024,256]{1,0:T(8,128)}, u32[]{:S(2)}, u32[]{:S(2)}) collective-permute-start(f32[1024,256]{1,0:T(8,128)} %add.222), channel_id=1, source_target_pairs={{0,2},{1,3},{2,4},{3,5},{4,6},{5,7},{6,8},{7,9},{8,10},{9,11},{10,... | collective-permute-start | bytes 3145736 | tf_op jit(solution)/shard_map/ppermute | solution.py:327
  203.3 1.9 copy-start.23
  205.2 1.9 copy-start.25
  207.1 30.0 %copy-start.9 = (f32[1024,256]{1,0:T(8,128)S(1)}, f32[1024,256]{1,0:T(8,128)}, u32[]{:S(2)}) copy-start(f32[1024,256]{1,0:T(8,128)} %copy-done.8) | copy-start | bytes 3145732
  237.1 2.5 copy-start.7
  242.0 44.9 %collective-permute-start.13 = (f32[1024,256]{1,0:T(8,128)}, f32[1024,256]{1,0:T(8,128)}, u32[]{:S(2)}, u32[]{:S(2)}) collective-permute-start(f32[1024,256]{1,0:T(8,128)} %add.224), channel_id=1, source_target_pairs={{0,2},{1,3},{2,4},{3,5},{4,6},{5,7},{6,8},{7,9},{8,10},{9,11},{10,... | collective-permute-start | bytes 3145736 | tf_op jit(solution)/shard_map/ppermute | solution.py:327
  242.0 44.9 %collective-permute-start.15 = (f32[1024,256]{1,0:T(8,128)}, f32[1024,256]{1,0:T(8,128)}, u32[]{:S(2)}, u32[]{:S(2)}) collective-permute-start(f32[1024,256]{1,0:T(8,128)} %add.225), channel_id=1, source_target_pairs={{0,14},{1,15},{2,0},{3,1},{4,2},{5,3},{6,4},{7,5},{8,6},{9,7},{10,... | collective-permute-start | bytes 3145736 | tf_op jit(solution)/shard_map/ppermute | solution.py:327
  244.8 42.1 %copy-start.20 = (f32[1024,256]{1,0:T(8,128)S(1)}, f32[1024,256]{1,0:T(8,128)}, u32[]{:S(2)}) copy-start(f32[1024,256]{1,0:T(8,128)} %copy-done.19) | copy-start | bytes 3145732
  285.8 2.9 copy-start.18
  288.6 1.9 copy-start.5
  288.6 2.5 copy-start.26
  293.0 12.8 %copy-start.2 = (bf16[2048,256]{1,0:T(8,128)(2,1)S(1)}, bf16[2048,256]{1,0:T(8,128)(2,1)}, u32[]{:S(2)}) copy-start(bf16[2048,256]{1,0:T(8,128)(2,1)} %e_ref.1) | copy-start | bytes 3145732
  (2 other events, 1.9 us)
Sparse Core Ops, SparseCore 0:
  10.2 43.7 all-gather.5
  57.2 57.0 all-gather.9
  116.9 58.6 all-gather.7
where the time goes:
time: 321 us; the launch traced here: 314 us
  Pallas kernels  135 us (42%)
  waiting for transfers between devices  80.9 us (25%)
  other arithmetic  31.2 us (10%)
  local copies, waits for them, and re-layouts  29.3 us (9%)
  starting transfers between devices  23.7 us (7%)
  between operations  14.5 us (5%)
    pallas_call x2, Pallas kernels, forward(): pl.pallas_call(functools.partial(forward_kernel, last, DP), grid=(C * nk,...  71 us
    all_gather x1, waiting for transfers between devices, program(): AT = lax.all_gather(rows(Ep.T), 'tp', axis=0, tiled=True)  44.8 us
    pallas_call x3, Pallas kernels, chip_parts(): pl.pallas_call(functools.partial(parts_kernel, nb), grid_spec=pltpu.Prefe...  27.5 us
    all_to_all x1, waiting for transfers between devices, program(): dc = lax.all_to_all(drs.reshape(K, TL, G, DL), 'tp', 2, 0, tiled=False)  19.7 us
    ppermute x14, starting transfers between devices, hop(): out[st] = lax.ppermute(b, 'tp', shift(st[1]))  17.8 us
    unnamed x66, local copies, waits for them, and re-layouts  15.8 us
    pallas_call x1, Pallas kernels, exchange(): pl.pallas_call(functools.partial(exchange_kernel, G), out_shape=jax.Shape...  15.5 us
    add x10, other arithmetic, add(): nxt[h, s, L] = b.astype(f32) + parts[s * (L - k), h]  14.9 us
  transfers between devices with their start and end apart: 20, of which 6 were waited for; matrix products, arithmetic and copies ran while one was open for 11% of the time, Pallas kernels for 40%

commit v1 on v0

--- a/solution.py
+++ b/solution.py
@@ -48,7 +48,7 @@
         ),
         out_shape=[jax.ShapeDtypeStruct((M, DL), dtype) for _ in blocks],
         cost_estimate=pl.CostEstimate(flops=4 * M * DL * FL * nb, bytes_accessed=8 << 20, transcendentals=0),
-        compiler_params=pltpu.CompilerParams(dimension_semantics=("arbitrary",), vmem_limit_bytes=40 << 20),
+        compiler_params=pltpu.CompilerParams(dimension_semantics=("arbitrary",), vmem_limit_bytes=62 << 20),
         name="chip_parts",
     )(idx, a, b, W, Wo.reshape(-1, FL))
     return dict(zip(blocks, outs))
@@ -63,15 +63,12 @@
     hi = d.astype(bf16)
     hi_ref[...] = hi
     lo_ref[...] = (d - hi.astype(f32)).astype(bf16)
-    x = lax.dot_general(hot, e_ref[...], (((0,), (0,)), ((), ())), preferred_element_type=f32)
 
     @pl.when(i == 0)
     def _():
-        acc_ref[...] = x
-
-    @pl.when(i > 0)
-    def _():
-        acc_ref[...] += x
+        acc_ref[...] = jnp.zeros(acc_ref.shape, f32)
+
+    acc_ref[...] += lax.dot_general(hot, e_ref[...], (((0,), (0,)), ((), ())), preferred_element_type=f32)
 
     @pl.when(i == pl.num_programs(0) - 1)
     def _():
@@ -97,7 +94,7 @@
                    jax.ShapeDtypeStruct((N, DL), bf16)],
         scratch_shapes=[pltpu.VMEM((N, DL), f32)],
         cost_estimate=pl.CostEstimate(flops=2 * V * N * (FL + DL), bytes_accessed=12 << 20, transcendentals=0),
-        compiler_params=pltpu.CompilerParams(dimension_semantics=("arbitrary",), vmem_limit_bytes=40 << 20),
+        compiler_params=pltpu.CompilerParams(dimension_semantics=("arbitrary",), vmem_limit_bytes=62 << 20),
         name="rowsums",
     )(ids, du, E)
 
@@ -182,15 +179,12 @@
     dw_ref[...] = (jnp.dot(n, dh_ref[...], preferred_element_type=f32)
                    + jnp.dot(n, dl_ref[...], preferred_element_type=f32))
     xo_ref[...] = jnp.dot(x, sr_ref[...], preferred_element_type=f32).T.astype(bf16)
-    up = lax.dot_general(w_ref[...], n, (((0,), (0,)), ((), ())), preferred_element_type=f32)
 
     @pl.when(j == 0)
     def _():
-        acc_ref[...] = up + up_ref[...] if last else up
-
-    @pl.when(j > 0)
-    def _():
-        acc_ref[...] += up
+        acc_ref[...] = up_ref[...] if last else jnp.zeros(acc_ref.shape, f32)
+
+    acc_ref[...] += lax.dot_general(w_ref[...], n, (((0,), (0,)), ((), ())), preferred_element_type=f32)
 
     if last:
         @pl.when(j == pl.num_programs(0) - 1)
@@ -210,16 +204,15 @@
             lax.fori_loop(0, u_ref.shape[0] // tb, step, 0)
 
 
-def forward(q, eb, rs, gcol, W, dh, dl, sr, up=None, ids=None, dw=None):
-    last = q == 1
-    DP, C, _, Vp = eb.shape
+def forward(row0, eb, rs, gcol, W, dh, dl, sr, up=None, ids=None, dw=None):
+    last = up is not None
+    DP, C, R, Vp = eb.shape
     V = DP * Vp
     D, FL = W.shape
-    Dq = D // (2 * C)
     kt = 512
-    nk = Dq // kt
+    nk = R // kt
     TS = sr.shape[1]
-    base = q * C * nk
+    base = row0 // kt
     one = pl.Buffered(1)
 
     def full(shape):
@@ -233,7 +226,7 @@
         full((V, FL)), full((V, FL)), full((V, TS)),
     ]
     args = [eb, rs, gcol, W, dh, dl, sr]
-    out_shape = [jax.ShapeDtypeStruct((D, FL), f32), jax.ShapeDtypeStruct((TS, D // 2), bf16)]
+    out_shape = [jax.ShapeDtypeStruct((D, FL), f32), jax.ShapeDtypeStruct((TS, C * R), bf16)]
     out_specs = [pl.BlockSpec((kt, FL), lambda j: (base + j, 0)), pl.BlockSpec((TS, kt), lambda j: (0, j))]
     scratch = []
     alias = {}
@@ -248,7 +241,7 @@
     else:
         out_shape.append(jax.ShapeDtypeStruct((FL, V), f32))
         out_specs.append(full((FL, V)))
-    flops = 2 * V * FL * (D // 2) * 3 + (2 * V * V * FL if last else 0)
+    flops = 2 * V * FL * C * R * 3 + (2 * V * V * FL if last else 0)
     return pl.pallas_call(
         functools.partial(forward_kernel, last, DP),
         grid=(C * nk,),
@@ -258,7 +251,7 @@
         scratch_shapes=scratch,
         input_output_aliases=alias,
         cost_estimate=pl.CostEstimate(flops=flops, bytes_accessed=30 << 20, transcendentals=0),
-        compiler_params=pltpu.CompilerParams(dimension_semantics=("arbitrary",), vmem_limit_bytes=(52 if last else 40) << 20),
+        compiler_params=pltpu.CompilerParams(dimension_semantics=("arbitrary",), vmem_limit_bytes=62 << 20),
         name="forward",
     )(*args)
 
@@ -297,7 +290,8 @@
         FL = W.shape[1]
         TL = T // G
         Vp = V // DP
-        Dq = D // (2 * C)
+        D1 = 3 * D // 4
+        R1, R2 = D1 // C, (D - D1) // C
         r = lax.axis_index('tp')
         grp = lax.axis_index('dp')
         z = r // C
@@ -314,8 +308,13 @@
         du_o = lax.ppermute(duf, 'tp', swap)
         Ws = lax.dynamic_index_in_dim(W.reshape(Z, C, DL, FL), 1 - c, 1, False)
         W_o = lax.ppermute(Ws, 'tp', swap)
+        el = E.astype(f32)
+        ssl = jnp.sum(el * el, axis=1)
+        ssl, _ = barrier((ssl, Ws))
+        ssg = exchange(G, ssl.reshape(V // 128, 128))
+        rs2 = lax.rsqrt(jnp.sum(ssg, axis=0) / D + EPS).reshape(1, V)
         gcol = gf.reshape(D, 1)
-        du_o, W_o, gcol = barrier((du_o, W_o, gcol))
+        du_o, W_o, gcol, rs2 = barrier((du_o, W_o, gcol, rs2))
         F = Z // 2
 
         streams = [(0, 1, F), (1, -1, F), (1, 1, F - 1), (0, -1, F - 1)]
@@ -349,17 +348,11 @@
         Wo1, _ = barrier((W_o, tuple(bufs.values())))
         p2 = chip(blocks(1), Wo1, f32)
 
-        el = E.astype(f32)
-        ssl = jnp.sum(el * el, axis=1)
-        ssl, _ = barrier((ssl, tuple(p2.values())))
-        ssg = exchange(G, ssl.reshape(V // 128, 128))
-        rs2 = lax.rsqrt(jnp.sum(ssg, axis=0) / D + EPS).reshape(1, V)
-
-        b1 = lax.dynamic_slice_in_dim(AT, c * Dq, Dq, axis=0)
-        b2 = lax.dynamic_slice_in_dim(AT, D // 2 + c * Dq, Dq, axis=0)
+        b1 = lax.dynamic_slice_in_dim(AT, c * R1, R1, axis=0)
+        b2 = lax.dynamic_slice_in_dim(AT, D1 + c * R2, R2, axis=0)
         b1, b2 = barrier((rows(b1), rows(b2)))
-        e1 = lax.all_gather(b1, ('dp', 'tp'), axis_index_groups=groups, axis=0, tiled=False).reshape(DP, C, Dq, Vp)
-        e2 = lax.all_gather(b2, ('dp', 'tp'), axis_index_groups=groups, axis=0, tiled=False).reshape(DP, C, Dq, Vp)
+        e1 = lax.all_gather(b1, ('dp', 'tp'), axis_index_groups=groups, axis=0, tiled=False).reshape(DP, C, R1, Vp)
+        e2 = lax.all_gather(b2, ('dp', 'tp'), axis_index_groups=groups, axis=0, tiled=False).reshape(DP, C, R2, Vp)
 
         bufs = add(moved, 1, p2, b2)
         Wo2, _ = barrier((W_o, tuple(bufs.values())))
@@ -370,7 +363,7 @@
         rst = jnp.sum(jnp.where(idx[:, None] == iota[None, :], rs2, 0.0), axis=1)
         idr = lax.dynamic_slice_in_dim(ids, r * TL, TL, axis=1).reshape(K * TL)
         sr = (iota[:, None] == idr[None, :]).astype(bf16)
-        idc = idx.reshape(N, 1)
+        idc = idf.reshape(N, 1)
         rs2, sr, idc, xl, rst = barrier((rs2, sr, idc, xl, rst))
 
         bufs = add(moved, 2, p3, xl)
@@ -378,14 +371,15 @@
         moved = hop(bufs)
         drs, _ = barrier((dres, tuple(bufs.values())))
         dc = lax.all_to_all(drs.reshape(K, TL, G, DL), 'tp', 2, 0, tiled=False)
-        dresc = dc.reshape(G, K, TL, DL).transpose(1, 0, 2, 3).reshape(N, DL)
         dw1, x1, up = forward(0, e1, rs2, gcol, W, dh, dl, sr)
         for k in range(3, F):
             bufs = add(moved, k, p3, x1)
             rs2, _ = barrier((rs2, tuple(bufs.values())))
             moved = hop(bufs)
-        dW, x2, u = forward(1, e2, rs2, gcol, W, dh, dl, sr, up, idc, dw1)
+        dW, x2, u = forward(D1, e2, rs2, gcol, W, dh, dl, sr, up, idc, dw1)
         moved = {st: barrier((b, x2))[0] for st, b in moved.items()}
+        dc, _ = barrier((dc, x2))
+        dresc = dc.reshape(G, K, TL, DL).transpose(1, 0, 2, 3).reshape(N, DL)
         add(moved, F, p3, x2)
         dn = jnp.concatenate([p3[(0, h)] + sum(b.astype(f32) for b in acc[h]) for h in (0, 1)], axis=0)
         xo = jnp.concatenate([x1, x2], axis=1).reshape(K, TL, D)

time: 321 us -> 322 us (level)
  waiting for transfers between devices: 80.9 us -> 53.4 us
  Pallas kernels: 135 us -> 154 us
  starting transfers between devices: 23.7 us -> 36.6 us
  local copies, waits for them, and re-layouts: 29.3 us -> 20.2 us
  other arithmetic: 31.2 us -> 37.1 us
    all_to_all x1, waiting for transfers between devices: 19.7 us -> 0.01 us  [program(): dc = lax.all_to_all(drs.reshape(K, TL, G, DL), 'tp', 2, 0, tiled=False)]
    all_to_all x1, starting transfers between devices: 5.21 us -> 19.7 us  [program(): dc = lax.all_to_all(drs.reshape(K, TL, G, DL), 'tp', 2, 0, tiled=False)]
    unnamed x66 -> x55, local copies, waits for them, and re-layouts: 15.8 us -> 3.74 us
    pallas_call x3, Pallas kernels: 27.5 us -> 36.2 us  [chip_parts(): pl.pallas_call(functools.partial(parts_kernel, nb), grid_spec=pltpu.Prefe...]
    pallas_call x1, Pallas kernels: 10.3 us -> 18.2 us  [rowsums(): pl.pallas_call(rowsum_kernel, grid=(V // vb,), in_specs=[pl.BlockSpec((1,...]
    add x10, other arithmetic: 14.9 us -> 22.1 us  [add(): nxt[h, s, L] = b.astype(f32) + parts[s * (L - k), h]]
    pallas_call x1, Pallas kernels: 15.5 us -> 9.13 us  [exchange(): pl.pallas_call(functools.partial(exchange_kernel, G), out_shape=jax.Shape...]
    pallas_call x2, Pallas kernels: 71 us -> 76.6 us  [forward(): pl.pallas_call(functools.partial(forward_kernel, last, DP), grid=(C * nk,...]
  transfers between devices with their start and end apart: 20 -> 20, of which waited for: 6 -> 3; matrix products, arithmetic and copies ran while one was open for 11% -> 13% of each run, Pallas kernels for 40% -> 44%
where the time goes in v1:
time: 322 us; the launch traced here: 316 us
  Pallas kernels  154 us (48%)
  waiting for transfers between devices  53.4 us (17%)
  other arithmetic  37.1 us (12%)
  starting transfers between devices  36.6 us (11%)
  local copies, waits for them, and re-layouts  20.2 us (6%)
  between operations  14.5 us (5%)
    pallas_call x2, Pallas kernels, forward(): pl.pallas_call(functools.partial(forward_kernel, last, DP), grid=(C * nk,...  76.6 us
    all_gather x1, waiting for transfers between devices, program(): AT = lax.all_gather(rows(Ep.T), 'tp', axis=0, tiled=True)  44.8 us
    pallas_call x3, Pallas kernels, chip_parts(): pl.pallas_call(functools.partial(parts_kernel, nb), grid_spec=pltpu.Prefe...  36.2 us
    add x10, other arithmetic, add(): nxt[h, s, L] = b.astype(f32) + parts[s * (L - k), h]  22.1 us
    all_to_all x1, starting transfers between devices, program(): dc = lax.all_to_all(drs.reshape(K, TL, G, DL), 'tp', 2, 0, tiled=False)  19.7 us
    pallas_call x1, Pallas kernels, rowsums(): pl.pallas_call(rowsum_kernel, grid=(V // vb,), in_specs=[pl.BlockSpec((1,...  18.2 us
    ppermute x14, starting transfers between devices, hop(): out[st] = lax.ppermute(b, 'tp', shift(st[1]))  16.2 us
    pallas_call x1, Pallas kernels, tail(): pl.pallas_call(functools.partial(tail_kernel, G), out_shape=(jax.ShapeDty...  13.9 us
  transfers between devices with their start and end apart: 20, of which 3 were waited for; matrix products, arithmetic and copies ran while one was open for 13% of the time, Pallas kernels for 44%

profile of v1, /device:TPU:21, one launch (start us, length us, event | category | flops | bytes accessed | tf_op | source)
XLA Modules:
  0.0 315.8 jit_solution(7060766651160637208)
XLA Ops:
  7.3 1.0 constant_dynamic-slice_fusion.3
  8.2 0.8 copy.36
  9.2 44.8 %all-gather.6.cloned.1.call-done = bf16[4096,512]{1,0:T(8,128)(2,1)} async-done(((bf16[256,512]{1,0:T(8,128)(2,1)}), bf16[4096,512]{1,0:T(8,128)(2,1)}) %all-gather.6.cloned.1.call-update) | async-done | bytes 4194320 | tf_op jit(solution)/shard_map/all_gather | solution.py:306
  54.0 2.7 constant_dynamic-slice_fusion.2
  56.7 1.9 constant_dynamic-slice_fusion.1
  58.7 3.9 %dynamic-slice_bitcast_fusion = bf16[8,256,768]{2,1,0:T(8,128)(2,1)} fusion(bf16[8,2,256,768]{3,2,1,0:T(8,128)(2,1)} %bitcast.71, s32[]{:T(128)S(6)} %select_n.41), kind=kLoop, calls=%fused_computation.5 | loop fusion | bytes 6291460 | tf_op jit(solution)/shard_map/jit(dynamic_index_in_dim)/squeeze | solution.py:309
  63.2 1.6 fusion
  65.1 9.1 %exchange.1 = f32[16,16,128]{2,1,0:T(8,128)S(1)} custom-call(f32[16,128]{1,0:T(8,128)S(1)} %bitcast.66), custom_call_target="tpu_custom_call" | custom-call | flops 1073741824 | bytes 1048576 | tf_op jit(solution)/shard_map/exchange/pallas_call | solution.py:126
  74.9 9.5 %chip_parts.3 = (bf16[1024,256]{1,0:T(8,128)(2,1)}, bf16[1024,256]{1,0:T(8,128)(2,1)}, bf16[1024,256]{1,0:T(8,128)(2,1)}, bf16[1024,256]{1,0:T(8,128)(2,1)}) custom-call(s32[8]{0:T(128)} %stack.96.idx_ref, bf16[2048,768]{1,0:T(8,128)(2,1)} %bitcast.72, bf16[2048,768]{1,0:T(8,128)(2,1)} %collective-permute-done.b_ref, bf16[4096,768]{1,0:T(8,128)(2,1)} %refs_3_.3, ...), custom_call_target="tpu_custom_call" | custom-call | flops 3221225472 | bytes 8388608 | tf_op jit(solution)/shard_map/chip_parts/pallas_call | solution.py:38
  84.4 1.5 collective-permute-start.5
  85.9 2.7 collective-permute-start.3
  88.6 0.9 fusion.5.refs_6_
  90.9 2.0 copy.31.refs_2_
  92.9 10.5 %chip_parts.4 = (f32[1024,256]{1,0:T(8,128)}, f32[1024,256]{1,0:T(8,128)}, f32[1024,256]{1,0:T(8,128)}, f32[1024,256]{1,0:T(8,128)}) custom-call(s32[8]{0:T(128)} %stack.97.idx_ref, bf16[2048,768]{1,0:T(8,128)(2,1)} %bitcast.73, bf16[2048,768]{1,0:T(8,128)(2,1)} %collective-permute-done.b_ref, bf16[4096,768]{1,0:T(8,128)(2,1)} %refs_3_.3, ...), custom_call_target="tpu_custom_call" | custom-call | flops 3221225472 | bytes 8388608 | tf_op jit(solution)/shard_map/chip_parts/pallas_call | solution.py:38
  103.4 5.7 %collective-permute-done.3 = bf16[1024,256]{1,0:T(8,128)(2,1)S(1)} collective-permute-done((bf16[1024,256]{1,0:T(8,128)(2,1)}, bf16[1024,256]{1,0:T(8,128)(2,1)S(1)}, u32[]{:S(2)}, u32[]{:S(2)}) %collective-permute-start.3) | collective-permute-done | bytes 524320 | tf_op jit(solution)/shard_map/ppermute | solution.py:326
  109.0 2.7 collective-permute-done.2
  111.8 2.5 convert_add_fusion
  114.3 1.1 collective-permute-start.9
  115.4 2.2 convert_add_fusion.1
  118.0 1.1 convert_add_fusion.2
  119.0 2.3 collective-permute-start.7
  121.4 1.1 convert_add_fusion.3
  122.9 16.3 %chip_parts.5 = (f32[1024,256]{1,0:T(8,128)}, f32[1024,256]{1,0:T(8,128)}, f32[1024,256]{1,0:T(8,128)}, f32[1024,256]{1,0:T(8,128)}, f32[1024,256]{1,0:T(8,128)}...) custom-call(s32[16]{0:T(128)} %stack.87.idx_ref, bf16[2048,768]{1,0:T(8,128)(2,1)} %bitcast.74, ...), custom_call_target="tpu_custom_call" | custom-call | flops 6442450944 | bytes 8388608 | tf_op jit(solution)/shard_map/chip_parts/pallas_call | solution.py:38
  139.2 2.3 select_reduce_fusion.1
  141.5 18.2 %rowsums.1 = (bf16[2048,768]{1,0:T(8,128)(2,1)}, bf16[2048,768]{1,0:T(8,128)(2,1)}, bf16[2048,256]{1,0:T(8,128)(2,1)}) custom-call(s32[1,2048]{1,0:T(1,128)} %bitcast.68, bf16[2048,768]{1,0:T(8,128)(2,1)} %bitcast.75, bf16[2048,256]{1,0:T(8,128)(2,1)} %e_ref.1), custom_call_target="tpu_custom_call" | custom-call | flops 8589934592 | bytes 12582912 | tf_op jit(solution)/shard_map/rowsums/pallas_call | solution.py:83
  159.6 1.3 copy.33.refs_8_
  161.0 2.7 add.217
  163.7 2.4 add.216
  166.1 2.5 add.215
  168.7 2.4 add.214
  171.1 2.5 collective-permute-start.11
  173.6 2.7 collective-permute-start.12
  176.5 1.3 copy.34
  177.8 19.7 %all-to-all-start = ((bf16[1,8,16,16,256]{4,2,1,0,3:T(8,128)(2,1)}), bf16[1,8,16,16,256]{4,2,1,0,3:T(8,128)(2,1)S(1)}, u32[]{:S(2)}, u32[]{:S(2)}) async-start(bf16[1,8,16,16,256]{4,2,1,0,3:T(8,128)(2,1)} %copy.34), calls=%async_computation | async-start | bytes 2097152 | tf_op jit(solution)/shard_map/all_to_all | solution.py:373
  197.6 47.0 %forward.2 = (f32[4096,768]{1,0:T(8,128)}, bf16[128,3072]{1,0:T(8,128)(2,1)}, f32[768,2048]{1,0:T(8,128)}) custom-call(bf16[4,2,1536,512]{3,2,1,0:T(8,128)(2,1)} %bitcast.93, f32[1,2048]{1,0:T(1,128)} %bitcast.88, f32[4096,1]{1,0:T(8,128)} %copy.31.refs_2_, bf16[4096,768]{1,0:T(8,128)(2,1)} %refs_3_.3, bf16[2048,768]{1,0:T(8,128)(2,1)} %get-tuple-element.101.refs_4_, ...), custom_call_target="tpu_custom_call" | custom-call | flops 28991029248 | bytes 31457280 | tf_op jit(solution)/shard_map/forward/pallas_call | solution.py:245
  244.6 2.8 add.219
  247.4 2.4 add.218
  249.8 1.4 collective-permute-start.13
  251.1 1.3 collective-permute-start.15
  252.4 29.6 %forward.3 = (f32[4096,768]{1,0:T(8,128)}, bf16[128,1024]{1,0:T(8,128)(2,1)}, bf16[2048,768]{1,0:T(8,128)(2,1)}) custom-call(bf16[4,2,512,512]{3,2,1,0:T(8,128)(2,1)} %bitcast.94, f32[1,2048]{1,0:T(1,128)} %bitcast.89, f32[4096,1]{1,0:T(8,128)} %copy.31.refs_2_, bf16[4096,768]{1,0:T(8,128)(2,1)} %refs_3_.3, ...), custom_call_target="tpu_custom_call", output_to_operand_aliasing={{0}: (9, {})} | custom-call | flops 16106127360 | bytes 31457280 | tf_op jit(solution)/shard_map/forward/pallas_call | solution.py:245
  282.6 0.9 copy-done.15
  283.5 1.0 pad_maximum_fusion.2
  285.1 1.7 add_add_fusion.1
  286.9 1.8 add_add_fusion
  288.7 1.1 reduce-precision_convert_fusion.1
  291.0 13.9 %tail.1 = (f32[16,18,128]{2,1,0:T(8,128)S(1)}, f32[2048,256]{1,0:T(8,128)S(1)}) custom-call(f32[18,128]{1,0:T(8,128)S(1)} %maximum_bitcast_fusion.s_ref, s32[1,2048]{1,0:T(1,128)S(1)} %bitcast.69, bf16[2048,768]{1,0:T(8,128)(2,1)S(1)} %pad_maximum_fusion.q_ref), custom_call_target="tpu_custom_call" | custom-call | flops 6442450944 | bytes 6291456 | tf_op jit(solution)/shard_map/tail/pallas_call | solution.py:158
  305.0 1.7 select_reduce_fusion
  307.4 1.7 fusion.3
  (100 shorter events, 7.1 us)
Async XLA Ops:
  7.2 46.9 %all-gather.6.cloned.1.call-start = ((), (), s32[]{:S(2)}) async-start(), calls=%async_computation.1 | async-start | bytes 4456448 | tf_op jit(solution)/shard_map/all_gather | solution.py:306
  9.1 188.4 %all-gather.10.cloned.1.call-start = ((), (), s32[]{:S(2)}) async-start(), calls=%async_computation.3 | async-start | bytes 14155776 | tf_op jit(solution)/shard_map/all_gather | solution.py:354
  58.6 193.8 %all-gather.8.cloned.1.call-start = ((), (), s32[]{:S(2)}) async-start(), calls=%async_computation.2 | async-start | bytes 4718592 | tf_op jit(solution)/shard_map/all_gather | solution.py:355
  58.7 4.2 %copy-start.2 = (bf16[8,256,768]{2,1,0:T(8,128)(2,1)S(1)}, bf16[8,256,768]{2,1,0:T(8,128)(2,1)}, u32[]{:S(2)}) copy-start(bf16[8,256,768]{2,1,0:T(8,128)(2,1)} %param.10) | copy-start | bytes 9437188
  58.7 6.1 %copy-start.23 = (bf16[4096]{0:T(1024)(128)(2,1)S(1)}, bf16[4096]{0:T(1024)(128)(2,1)}, u32[]{:S(2)}) copy-start(bf16[4096]{0:T(1024)(128)(2,1)} %param.8) | copy-start | bytes 24580
  58.7 6.2 %copy-start.20 = (s32[8,256]{1,0:T(8,128)S(1)}, s32[8,256]{1,0:T(8,128)}, u32[]{:S(2)}) copy-start(s32[8,256]{1,0:T(8,128)} %param.6) | copy-start | bytes 24580
  62.7 12.3 %collective-permute-start.1 = (bf16[8,256,768]{2,1,0:T(8,128)(2,1)}, bf16[8,256,768]{2,1,0:T(8,128)(2,1)}, u32[]{:S(2)}, u32[]{:S(2)}) collective-permute-start(bf16[8,256,768]{2,1,0:T(8,128)(2,1)} %dynamic-slice_bitcast_fusion), channel_id=1, source_target_pairs={{0,1},{1,0},{2,3},{3,2},{4,5},{5,4},{6,7},{7,6},{8,9},{9,8},{10,11... | collective-permute-start | bytes 9437192 | tf_op jit(solution)/shard_map/ppermute | solution.py:310
  62.9 12.0 %collective-permute-start = (bf16[2048,768]{1,0:T(8,128)(2,1)S(1)}, bf16[2048,768]{1,0:T(8,128)(2,1)}, u32[]{:S(2)}, u32[]{:S(2)}) collective-permute-start(bf16[2048,768]{1,0:T(8,128)(2,1)S(1)} %bitcast.76), channel_id=1, source_target_pairs={{0,1},{1,0},{2,3},{3,2},{4,5},{5,4},{6,7},{7,6},{8,9},{9,8},{10,11... | collective-permute-start | bytes 9437192 | tf_op jit(solution)/shard_map/ppermute | solution.py:308
  74.9 64.3 %copy-start.21 = (f32[16,128]{1,0:T(8,128)}, f32[16,128]{1,0:T(8,128)S(1)}, u32[]{:S(2)}) copy-start(f32[16,128]{1,0:T(8,128)S(1)} %add_rsqrt_fusion) | copy-start | bytes 24580
  84.4 18.9 %collective-permute-start.5 = (bf16[1024,256]{1,0:T(8,128)(2,1)}, bf16[1024,256]{1,0:T(8,128)(2,1)}, u32[]{:S(2)}, u32[]{:S(2)}) collective-permute-start(bf16[1024,256]{1,0:T(8,128)(2,1)} %get-tuple-element.72), channel_id=1, source_target_pairs={{0,14},{1,15},{2,0},{3,1},{4,2},{5,3},{6,4},{7,5},{8,6},{9,7},{10,... | collective-permute-start | bytes 1572872 | tf_op jit(solution)/shard_map/ppermute | solution.py:326
  85.9 17.4 %collective-permute-start.4 = (bf16[1024,256]{1,0:T(8,128)(2,1)}, bf16[1024,256]{1,0:T(8,128)(2,1)S(1)}, u32[]{:S(2)}, u32[]{:S(2)}) collective-permute-start(bf16[1024,256]{1,0:T(8,128)(2,1)} %get-tuple-element.71), channel_id=1, source_target_pairs={{0,2},{1,3},{2,4},{3,5},{4,6},{5,7},{6,8},{7,9},{8,10},{9,11},{10,... | collective-permute-start | bytes 1572872 | tf_op jit(solution)/shard_map/ppermute | solution.py:326
  85.9 23.1 %collective-permute-start.3 = (bf16[1024,256]{1,0:T(8,128)(2,1)}, bf16[1024,256]{1,0:T(8,128)(2,1)S(1)}, u32[]{:S(2)}, u32[]{:S(2)}) collective-permute-start(bf16[1024,256]{1,0:T(8,128)(2,1)} %get-tuple-element.70), channel_id=1, source_target_pairs={{0,14},{1,15},{2,0},{3,1},{4,2},{5,3},{6,4},{7,5},{8,6},{9,7},{10,... | collective-permute-start | bytes 1572872 | tf_op jit(solution)/shard_map/ppermute | solution.py:326
  88.6 23.2 %collective-permute-start.2 = (bf16[1024,256]{1,0:T(8,128)(2,1)}, bf16[1024,256]{1,0:T(8,128)(2,1)S(1)}, u32[]{:S(2)}, u32[]{:S(2)}) collective-permute-start(bf16[1024,256]{1,0:T(8,128)(2,1)} %get-tuple-element.68), channel_id=1, source_target_pairs={{0,2},{1,3},{2,4},{3,5},{4,6},{5,7},{6,8},{7,9},{8,10},{9,11},{10,... | collective-permute-start | bytes 1572872 | tf_op jit(solution)/shard_map/ppermute | solution.py:326
  89.5 49.6 %copy-start = (s32[1,2,8,128]{3,1,2,0:T(2,128)}, s32[1,2,8,128]{3,1,2,0:T(2,128)S(1)}, u32[]{:S(2)}) copy-start(s32[1,2,8,128]{3,1,2,0:T(2,128)S(1)} %copy.38) | copy-start | bytes 24580
  103.3 12.1 %copy-start.12 = (f32[1024,256]{1,0:T(8,128)S(1)}, f32[1024,256]{1,0:T(8,128)}, u32[]{:S(2)}) copy-start(f32[1024,256]{1,0:T(8,128)} %get-tuple-element.78) | copy-start | bytes 3145732
  103.4 8.4 %copy-start.18 = (bf16[1024,256]{1,0:T(8,128)(2,1)}, bf16[1024,256]{1,0:T(8,128)(2,1)S(1)}, u32[]{:S(2)}) copy-start(bf16[1024,256]{1,0:T(8,128)(2,1)S(1)} %collective-permute-done.4) | copy-start | bytes 1572868
  109.0 2.7 copy-start.16
  111.8 6.2 %copy-start.11 = (f32[1024,256]{1,0:T(8,128)S(1)}, f32[1024,256]{1,0:T(8,128)}, u32[]{:S(2)}) copy-start(f32[1024,256]{1,0:T(8,128)} %get-tuple-element.76) | copy-start | bytes 3145732
  114.3 3.7 %copy-start.17 = (bf16[1024,256]{1,0:T(8,128)(2,1)S(1)}, bf16[1024,256]{1,0:T(8,128)(2,1)}, u32[]{:S(2)}) copy-start(bf16[1024,256]{1,0:T(8,128)(2,1)} %copy-done.16) | copy-start | bytes 1572868
  114.3 46.7 %collective-permute-start.9 = (f32[1024,256]{1,0:T(8,128)}, f32[1024,256]{1,0:T(8,128)S(1)}, u32[]{:S(2)}, u32[]{:S(2)}) collective-permute-start(f32[1024,256]{1,0:T(8,128)} %convert_add_fusion), channel_id=1, source_target_pairs={{0,14},{1,15},{2,0},{3,1},{4,2},{5,3},{6,4},{7,5},{8,6},{9,7},{10,... | collective-permute-start | bytes 3145736 | tf_op jit(solution)/shard_map/ppermute | solution.py:326
  115.4 6.0 %copy-start.10 = (f32[1024,256]{1,0:T(8,128)S(1)}, f32[1024,256]{1,0:T(8,128)}, u32[]{:S(2)}) copy-start(f32[1024,256]{1,0:T(8,128)} %get-tuple-element.74) | copy-start | bytes 3145732
  117.6 46.1 %collective-permute-start.8 = (f32[1024,256]{1,0:T(8,128)}, f32[1024,256]{1,0:T(8,128)}, u32[]{:S(2)}, u32[]{:S(2)}) collective-permute-start(f32[1024,256]{1,0:T(8,128)} %convert_add_fusion.1), channel_id=1, source_target_pairs={{0,2},{1,3},{2,4},{3,5},{4,6},{5,7},{6,8},{7,9},{8,10},{9,11},{10,... | collective-permute-start | bytes 3145736 | tf_op jit(solution)/shard_map/ppermute | solution.py:326
  119.0 47.1 %collective-permute-start.7 = (f32[1024,256]{1,0:T(8,128)}, f32[1024,256]{1,0:T(8,128)}, u32[]{:S(2)}, u32[]{:S(2)}) collective-permute-start(f32[1024,256]{1,0:T(8,128)} %convert_add_fusion.2), channel_id=1, source_target_pairs={{0,14},{1,15},{2,0},{3,1},{4,2},{5,3},{6,4},{7,5},{8,6},{9,7},{10,... | collective-permute-start | bytes 3145736 | tf_op jit(solution)/shard_map/ppermute | solution.py:326
  122.5 46.1 %collective-permute-start.6 = (f32[1024,256]{1,0:T(8,128)}, f32[1024,256]{1,0:T(8,128)}, u32[]{:S(2)}, u32[]{:S(2)}) collective-permute-start(f32[1024,256]{1,0:T(8,128)} %convert_add_fusion.3), channel_id=1, source_target_pairs={{0,2},{1,3},{2,4},{3,5},{4,6},{5,7},{6,8},{7,9},{8,10},{9,11},{10,... | collective-permute-start | bytes 3145736 | tf_op jit(solution)/shard_map/ppermute | solution.py:326
  159.6 4.0 %copy-start.8 = (f32[1024,256]{1,0:T(8,128)S(1)}, f32[1024,256]{1,0:T(8,128)}, u32[]{:S(2)}) copy-start(f32[1024,256]{1,0:T(8,128)} %get-tuple-element.87) | copy-start | bytes 3145732
  163.7 2.4 copy-start.7
  166.1 2.5 copy-start.6
  168.6 7.6 %copy-start.9 = (bf16[8,16,4096]{2,1,0:T(8,128)(2,1)S(1)}, bf16[8,16,4096]{2,1,0:T(8,128)(2,1)}, u32[]{:S(2)}) copy-start(bf16[8,16,4096]{2,1,0:T(8,128)(2,1)} %param.11) | copy-start | bytes 3145732
  171.1 73.6 %collective-permute-start.11 = (f32[1024,256]{1,0:T(8,128)}, f32[1024,256]{1,0:T(8,128)}, u32[]{:S(2)}, u32[]{:S(2)}) collective-permute-start(f32[1024,256]{1,0:T(8,128)} %add.215), channel_id=1, source_target_pairs={{0,14},{1,15},{2,0},{3,1},{4,2},{5,3},{6,4},{7,5},{8,6},{9,7},{10,... | collective-permute-start | bytes 3145736 | tf_op jit(solution)/shard_map/ppermute | solution.py:326
  173.6 73.8 %collective-permute-start.10 = (f32[1024,256]{1,0:T(8,128)}, f32[1024,256]{1,0:T(8,128)}, u32[]{:S(2)}, u32[]{:S(2)}) collective-permute-start(f32[1024,256]{1,0:T(8,128)} %add.214), channel_id=1, source_target_pairs={{0,2},{1,3},{2,4},{3,5},{4,6},{5,7},{6,8},{7,9},{8,10},{9,11},{10,... | collective-permute-start | bytes 3145736 | tf_op jit(solution)/shard_map/ppermute | solution.py:326
  173.6 111.0 %collective-permute-start.12 = (f32[1024,256]{1,0:T(8,128)}, f32[1024,256]{1,0:T(8,128)}, u32[]{:S(2)}, u32[]{:S(2)}) collective-permute-start(f32[1024,256]{1,0:T(8,128)} %add.217), channel_id=1, source_target_pairs={{0,14},{1,15},{2,0},{3,1},{4,2},{5,3},{6,4},{7,5},{8,6},{9,7},{10,... | collective-permute-start | bytes 3145736 | tf_op jit(solution)/shard_map/ppermute | solution.py:326
  176.2 110.6 %collective-permute-start.14 = (f32[1024,256]{1,0:T(8,128)}, f32[1024,256]{1,0:T(8,128)}, u32[]{:S(2)}, u32[]{:S(2)}) collective-permute-start(f32[1024,256]{1,0:T(8,128)} %add.216), channel_id=1, source_target_pairs={{0,2},{1,3},{2,4},{3,5},{4,6},{5,7},{6,8},{7,9},{8,10},{9,11},{10,... | collective-permute-start | bytes 3145736 | tf_op jit(solution)/shard_map/ppermute | solution.py:326
  177.8 104.2 %all-to-all-start = ((bf16[1,8,16,16,256]{4,2,1,0,3:T(8,128)(2,1)}), bf16[1,8,16,16,256]{4,2,1,0,3:T(8,128)(2,1)S(1)}, u32[]{:S(2)}, u32[]{:S(2)}) async-start(bf16[1,8,16,16,256]{4,2,1,0,3:T(8,128)(2,1)} %copy.34), calls=%async_computation | async-start | bytes 2097152 | tf_op jit(solution)/shard_map/all_to_all | solution.py:373
  244.6 2.8 copy-start.5
  249.8 34.8 %collective-permute-start.13 = (f32[1024,256]{1,0:T(8,128)}, f32[1024,256]{1,0:T(8,128)}, u32[]{:S(2)}, u32[]{:S(2)}) collective-permute-start(f32[1024,256]{1,0:T(8,128)} %add.218), channel_id=1, source_target_pairs={{0,2},{1,3},{2,4},{3,5},{4,6},{5,7},{6,8},{7,9},{8,10},{9,11},{10,... | collective-permute-start | bytes 3145736 | tf_op jit(solution)/shard_map/ppermute | solution.py:326
  251.1 33.4 %collective-permute-start.15 = (f32[1024,256]{1,0:T(8,128)}, f32[1024,256]{1,0:T(8,128)}, u32[]{:S(2)}, u32[]{:S(2)}) collective-permute-start(f32[1024,256]{1,0:T(8,128)} %add.219), channel_id=1, source_target_pairs={{0,14},{1,15},{2,0},{3,1},{4,2},{5,3},{6,4},{7,5},{8,6},{9,7},{10,... | collective-permute-start | bytes 3145736 | tf_op jit(solution)/shard_map/ppermute | solution.py:326
  282.3 1.1 copy-start.15
  282.3 1.2 copy-start.19
  283.5 1.6 copy-start.14
  284.6 2.3 copy-start.13
  286.9 1.9 copy-start.4
  290.3 0.7 copy-start.1
  291.0 16.4 %copy-start.3 = (bf16[2048,256]{1,0:T(8,128)(2,1)S(1)}, bf16[2048,256]{1,0:T(8,128)(2,1)}, u32[]{:S(2)}) copy-start(bf16[2048,256]{1,0:T(8,128)(2,1)} %e_ref.1) | copy-start | bytes 3145732
  291.0 16.4 %copy-start.22 = (f32[16,128]{1,0:T(8,128)S(1)}, f32[16,128]{1,0:T(8,128)}, u32[]{:S(2)}) copy-start(f32[16,128]{1,0:T(8,128)} %copy-done.21) | copy-start | bytes 24580
Sparse Core Ops, SparseCore 0:
  10.2 43.7 all-gather.5
  58.7 74.7 all-gather.9
  135.6 41.0 all-gather.7
